TPU v7x, 128 devices: a whole 4x4x4 slice. The times are simulated.
128 devices in a mesh: seq: 16 (over x, z), head: 8 (over y, core).
Axes of the slice: x: 4, y: 4, z: 4, core: 2. Of those that a mesh axis runs over, the one named last changes fastest.
Arguments:
- latent: float32 [4096, 128], P('seq'), may hold values from -6 to 6
- w_in: bfloat16 [128, 3072], replicated, may hold values from -0.5 to 0.5
- w_query: bfloat16 [3072, 3072], P(None, 'head'), may hold values from -0.109375 to 0.109375
- w_key: bfloat16 [3072, 3072], P(None, 'head'), may hold values from -0.109375 to 0.109375
- w_value: bfloat16 [3072, 3072], P(None, 'head'), may hold values from -0.109375 to 0.109375
- w_attn_out: bfloat16 [3072, 3072], P('head'), may hold values from -0.109375 to 0.109375
- w_up: bfloat16 [3072, 12288], P('seq', 'head'), may hold values from -0.109375 to 0.109375
- w_down: bfloat16 [12288, 3072], P('head', 'seq'), may hold values from -0.0546875 to 0.0546875
- w_final: bfloat16 [3072, 256], replicated, may hold values from -0.109375 to 0.109375
- gain_attn: float32 [3072], replicated, may hold values from 0.5 to 1.5
- gain_mlp: float32 [3072], replicated, may hold values from 0.5 to 1.5
- gain_final: float32 [3072], replicated, may hold values from 0.5 to 1.5
Outputs:
- restored: float32 [4096, 128], P('seq')
All inputs are finite; a program needn't handle non-finite values.
Results may differ from a plain program's by a relative error of at most 0.013.
Values may be sent and summed in bfloat16 or wider, within the bound.
A program may use at most 192 MiB of HBM per device.

v0:
```python
import jax
import jax.numpy as jnp
from jax import lax
from jax.sharding import PartitionSpec as P

D = 3072
HEAD_DIM = 128
C = 128
ITERS = 2


EPSILON = 1e-05


def rows_first(arrays, axis, dims):
    turned = [jnp.moveaxis(a, dim, 0) for a, dim in zip(arrays, dims)]
    both = jnp.concatenate([t.reshape(len(t), -1) for t in turned], axis=1)
    whole, at, done = (lax.all_gather(both, axis, axis=0, tiled=True), 0, [])
    for t, dim in zip(turned, dims):
        section = whole[:, at : at + t[0].size].reshape(-1, *t.shape[1:])
        done.append(jnp.moveaxis(section, 0, dim))
        at += t[0].size
    return tuple(done)


def in_one_piece(arrays, axis, dim, along):
    widths = [a.shape[along] for a in arrays]
    both = jnp.concatenate(arrays, axis=along)
    whole = lax.all_gather(both, axis, axis=dim, tiled=True)
    return tuple(jnp.split(whole, [sum(widths[:k]) for k in range(1, len(widths))], axis=along))


def filled_up(lines, count):
    spare = -lines.shape[0] % count
    if not spare:
        return lines
    return jnp.concatenate([lines, jnp.zeros((spare, *lines.shape[1:]), lines.dtype)])


def sum_by_parts(shard, axis):
    lines = shard.reshape(-1, *shard.shape[1:][-1:])
    padded = filled_up(lines, lax.axis_size(axis))
    own = lax.psum_scatter(padded, axis, scatter_dimension=0, tiled=True)
    whole = lax.all_gather(own, axis, axis=0, tiled=True)
    return whole[: len(lines)].reshape(shard.shape)


def passed_along(value, axis, steps):
    count = lax.axis_size(axis)
    leading, last = (max(0, -steps), min(count, count - steps))
    return lax.ppermute(value, axis, [(source, source + steps) for source in range(leading, last)])


def swapped(block, axis, bit):
    count = lax.axis_size(axis)
    route = []
    for low in range(count):
        high = low | 1 << bit
        if high != low and high < count:
            route += [(low, high), (high, low)]
    return lax.ppermute(block, axis, route)


def layer_norm(stream, gain):
    center = stream - jnp.mean(stream, axis=-1, keepdims=True)
    spread = jnp.mean(center * center, axis=-1, keepdims=True)
    return center * lax.rsqrt(spread + EPSILON) * gain


def sinusoid(positions, model_width):
    pair_count = model_width // 2
    frequency = jnp.exp(
        -jnp.log(10000.0) * 2.0 * jnp.arange(pair_count).astype(jnp.float32) / model_width
    )
    angles = positions[:, None] * frequency[None, :]
    return jnp.concatenate([jnp.sin(angles), jnp.cos(angles)], axis=1)


def per_device(
    latent,
    w_in,
    w_query,
    w_key,
    w_value,
    w_attn_out,
    w_up,
    w_down,
    w_final,
    gain_attn,
    gain_mlp,
    gain_final,
):
    seq_count = lax.axis_size("seq")
    my_index = lax.axis_index("seq")
    row_count = latent.shape[0]
    local_heads = w_query.shape[1] // HEAD_DIM
    up_full, down_full = rows_first((w_up, w_down), "seq", (0, 1))
    positions_int = my_index * row_count + jnp.arange(row_count, dtype=jnp.int32)
    embedding = sinusoid(positions_int.astype(jnp.float32), D)
    query_last = jnp.max(positions_int)
    current = latent
    for step_index in range(ITERS):
        stream_in = (
            jnp.dot(current.astype(jnp.bfloat16), w_in, preferred_element_type=jnp.float32)
            + embedding
        )
        normed = layer_norm(stream_in, gain_attn).astype(jnp.bfloat16)
        queries = (
            jnp.dot(normed, w_query, preferred_element_type=jnp.float32) * HEAD_DIM ** (-0.5)
        ).astype(jnp.bfloat16)
        queries = queries.reshape(row_count, local_heads, HEAD_DIM)
        key_rows = jnp.dot(normed, w_key, preferred_element_type=jnp.float32).astype(jnp.bfloat16)
        value_rows = jnp.dot(normed, w_value, preferred_element_type=jnp.float32).astype(
            jnp.bfloat16
        )
        initial = (
            jnp.zeros((local_heads, row_count), jnp.float32),
            jnp.zeros((local_heads, row_count, HEAD_DIM), jnp.float32),
        )
        block_keys, block_values = in_one_piece((key_rows, value_rows), "seq", 0, 1)
        attend_span_rows = block_keys.shape[0]
        key_positions = jnp.arange(attend_span_rows, dtype=jnp.int32)
        attend_key_positions = key_positions

        def update(state_in):
            scores = jnp.einsum(
                "qhd,khd->hqk",
                queries,
                block_keys.reshape(attend_span_rows, local_heads, HEAD_DIM),
                preferred_element_type=jnp.float32,
            )
            visible = attend_key_positions[None, None, :] <= positions_int[None, :, None]
            weights_now = jnp.where(visible, jnp.exp(jnp.where(visible, scores, 0.0)), 0.0)
            totals_new = jnp.sum(weights_now, axis=-1)
            weighted_new = jnp.einsum(
                "hqk,khd->hqd",
                weights_now.astype(jnp.bfloat16),
                block_values.reshape(attend_span_rows, local_heads, HEAD_DIM),
                preferred_element_type=jnp.float32,
            )
            return (totals_new, weighted_new)

        totals, weighted = lax.cond(
            jnp.min(attend_key_positions) <= query_last, update, lambda state_in: state_in, initial
        )
        attended = (
            (weighted / totals[..., None])
            .transpose(1, 0, 2)
            .reshape(row_count, local_heads * HEAD_DIM)
            .astype(jnp.bfloat16)
        )
        stream_attn = stream_in + sum_by_parts(
            jnp.dot(attended, w_attn_out, preferred_element_type=jnp.float32).astype(jnp.bfloat16),
            "head",
        ).astype(jnp.float32)
        normed_mlp = layer_norm(stream_attn, gain_mlp).astype(jnp.bfloat16)
        hidden = jax.nn.gelu(
            jnp.dot(normed_mlp, up_full, preferred_element_type=jnp.float32), approximate=True
        ).astype(jnp.bfloat16)
        stream_mlp = stream_attn + sum_by_parts(
            jnp.dot(hidden, down_full, preferred_element_type=jnp.float32).astype(jnp.bfloat16),
            "head",
        ).astype(jnp.float32)
        final_normed = layer_norm(stream_mlp, gain_final).astype(jnp.bfloat16)
        params_out = jnp.dot(final_normed, w_final, preferred_element_type=jnp.float32)
        from_before = passed_along(params_out[row_count - 1 :], "seq", 1)
        shifted = jnp.concatenate([from_before, params_out[: row_count - 1]], axis=0)
        current = latent * jnp.exp(jnp.tanh(shifted[:, C:])) + shifted[:, :C]
    result = current[::-1]
    for bit_number in range(seq_count.bit_length() - 1):
        result = swapped(result.astype(jnp.bfloat16), "seq", bit_number).astype(result.dtype)
    return result


def solution(mesh):
    in_specs = (
        P("seq", None),
        P(),
        P(None, "head"),
        P(None, "head"),
        P(None, "head"),
        P("head", None),
        P("seq", "head"),
        P("head", "seq"),
        P(),
        P(),
        P(),
        P(),
    )
    out_specs = P("seq", None)
    return jax.shard_map(
        per_device, mesh=mesh, in_specs=in_specs, out_specs=out_specs, check_vma=False
    )
```

profile of v0, /device:TPU:1, one launch (start us, length us, event | category | flops | bytes accessed | tf_op | source)
XLA Modules:
  0.0 660.6 jit_solution(12850073921208557508)
XLA Ops:
  7.2 5.5 multiply_sine_fusion
  16.1 1.1 copy-done.30
  17.2 1.0 convolution_convert_fusion.4
  18.2 1.2 copy-done.32
  19.5 1.0 convolution_convert_fusion.5
  20.5 0.8 pad_maximum_fusion.2
  22.6 3.8 fusion.78
  26.4 59.5 %all-gather.8.cloned.1.call-done = bf16[4096,768]{1,0:T(8,128)(2,1)} async-done(((bf16[256,768]{1,0:T(8,128)(2,1)}), bf16[4096,768]{1,0:T(8,128)(2,1)}) %all-gather.8.cloned.1.call-update) | async-done | bytes 6291472 | tf_op jit(solution)/shard_map/all_gather | solution.py:29
  85.9 33.3 %conditional.2 = (f32[3,256]{1,0:T(4,128)}, f32[3,256,128]{1,2,0:T(8,128)S(1)}) conditional(s32[]{:T(128)} %convert_element_type.129, () %tuple.21, (s32[4096]{0:T(1024)S(1)}, s32[256]{0:T(256)}, bf16[256,384]{1,0:T(8,128)(2,1)}, bf16[4096,768]{1,0:T(8,128)(2,1)}) %tuple.22), branch_computations={%region_3.0_spmd, %region_4.6_spmd} | conditional | flops 1630534912 | bytes 78340224 | solution.py:143
  86.1 8.7 %copy.22 = bf16[4096,768]{0,1:T(8,128)(2,1)} copy(bf16[4096,768]{1,0:T(8,128)(2,1)} %get-tuple-element.48) | data formatting | bytes 12582912 | tf_op jit(solution)/shard_map
  94.7 6.4 fusion.114
  101.1 1.7 broadcast_compare_fusion
  102.9 9.7 %fusion.1 = (f32[3,256]{1,0:T(4,128)}, f32[3,256,4096]{2,1,0:T(8,128)}) fusion(pred[256,4096]{1,0:T(8,128)(4,1)} %broadcast_compare_fusion, bf16[256,3,128]{0,2,1:T(8,128)(2,1)S(1)} %bitcast.50, bf16[4096,3,128]{0,2,1:T(8,128)(2,1)} %bitcast.43), kind=kOutput, calls=%fused_computation.2 | convolution fusion | flops 814742784 | bytes 16976896 | tf_op jit(solution)/shard_map/cond/branch_1_fun/qhd,khd->hqk/dot_general | solution.py:126
  112.6 6.6 fusion.2
  119.2 0.7 divide_convert_fusion.1
  119.9 2.2 convolution_convert_fusion.1
  122.2 30.1 %reduce-scatter.5.cloned.1.call-done = bf16[32,3072]{1,0:T(8,128)(2,1)} async-done(((bf16[256,3072]{1,0:T(8,128)(2,1)}), bf16[32,3072]{1,0:T(8,128)(2,1)}) %reduce-scatter.5.cloned.1.call-update) | async-done | bytes 196624 | tf_op jit(solution)/shard_map/reduce_scatter | solution.py:43
  152.4 2.4 pad_maximum_fusion.1
  154.9 25.4 %all-gather.10.cloned.1.call-done = bf16[256,3072]{1,0:T(8,128)(2,1)} async-done(((bf16[32,3072]{1,0:T(8,128)(2,1)}), bf16[256,3072]{1,0:T(8,128)(2,1)}) %all-gather.10.cloned.1.call-update) | async-done | bytes 1572880 | tf_op jit(solution)/shard_map/all_gather | solution.py:44
  180.3 2.7 fusion.113
  183.1 1.7 copy-done.1
  185.2 118.9 %all-gather.12.cloned.1.call-done = bf16[3072,3072]{1,0:T(8,128)(2,1)} async-done(((bf16[192,3072]{1,0:T(8,128)(2,1)}), bf16[3072,3072]{1,0:T(8,128)(2,1)}) %all-gather.12.cloned.1.call-update) | async-done | bytes 18874384 | tf_op jit(solution)/shard_map/all_gather | solution.py:18
  304.1 13.7 %fusion.22 = bf16[256,3072]{1,0:T(8,128)(2,1)} fusion(bf16[3072,3072]{1,0:T(8,128)(2,1)} %all-gather.12.cloned.1.call-done, f32[256,3072]{1,0:T(8,128)} %copy-done.1, f32[3072]{0:T(1024)S(1)} %copy-done.34, f32[256]{0:T(256)S(1)} %add_rsqrt_fusion.4, f32[256]{0:T(256)S(1)} %broadcast_multiply_fusion.4), kind=kOutput, calls=%fused_computation.26 | convolution fusion | flops 4839309312 | bytes 23607296 | tf_op jit(solution)/shard_map/dot_general | solution.py:161
  317.8 30.1 %reduce-scatter.7.cloned.1.call-done = bf16[32,3072]{1,0:T(8,128)(2,1)} async-done(((bf16[256,3072]{1,0:T(8,128)(2,1)}), bf16[32,3072]{1,0:T(8,128)(2,1)}) %reduce-scatter.7.cloned.1.call-update) | async-done | bytes 196624 | tf_op jit(solution)/shard_map/reduce_scatter | solution.py:43
  348.2 27.5 %all-gather.14.cloned.1.call-done = bf16[256,3072]{1,0:T(8,128)(2,1)} async-done(((bf16[32,3072]{1,0:T(8,128)(2,1)}), bf16[256,3072]{1,0:T(8,128)(2,1)}) %all-gather.14.cloned.1.call-update) | async-done | bytes 1572880 | tf_op jit(solution)/shard_map/all_gather | solution.py:44
  375.7 2.9 fusion.76
  380.3 0.8 fusion.56
  381.1 3.3 collective-permute-start
  384.4 0.7 collective-permute-done
  385.1 0.7 fusion.117
  387.4 1.2 copy-done.31
  388.6 1.0 convolution_convert_fusion.2
  389.6 1.2 copy-done.33
  390.8 1.0 convolution_convert_fusion.3
  391.9 0.8 pad_maximum_fusion.3
  392.7 3.1 fusion.79
  395.9 59.6 %all-gather.16.cloned.1.call-done = bf16[4096,768]{1,0:T(8,128)(2,1)} async-done(((bf16[256,768]{1,0:T(8,128)(2,1)}), bf16[4096,768]{1,0:T(8,128)(2,1)}) %all-gather.16.cloned.1.call-update) | async-done | bytes 6291472 | tf_op jit(solution)/shard_map/all_gather | solution.py:29
  455.5 32.9 %conditional.3 = (f32[3,256]{1,0:T(4,128)S(1)}, f32[3,256,128]{1,2,0:T(8,128)S(1)}) conditional(s32[]{:T(128)} %convert_element_type.129, () %tuple.23, (s32[4096]{0:T(1024)S(1)}, s32[256]{0:T(256)S(1)}, bf16[256,384]{1,0:T(8,128)(2,1)S(1)}, bf16[4096,768]{1,0:T(8,128)(2,1)}) %tuple.67), branch_computations={%region_14.15_spmd, %region_15.0_spmd} | conditional | flops 1630534912 | bytes 77549640 | solution.py:143
  455.5 8.9 %copy.25 = bf16[4096,768]{0,1:T(8,128)(2,1)} copy(bf16[4096,768]{1,0:T(8,128)(2,1)} %get-tuple-element.52) | data formatting | bytes 12582912 | tf_op jit(solution)/shard_map
  464.3 6.3 fusion.115
  470.7 1.6 broadcast_compare_fusion.1
  472.5 9.1 %fusion.8 = (f32[3,256]{1,0:T(4,128)S(1)}, f32[3,256,4096]{2,1,0:T(8,128)}) fusion(pred[256,4096]{1,0:T(8,128)(4,1)} %broadcast_compare_fusion.1, bf16[256,3,128]{0,2,1:T(8,128)(2,1)S(1)} %bitcast.51, bf16[4096,3,128]{0,2,1:T(8,128)(2,1)} %bitcast.44), kind=kOutput, calls=%fused_computation.10 | convolution fusion | flops 814742784 | bytes 16976896 | tf_op jit(solution)/shard_map/cond/branch_1_fun/qhd,khd->hqk/dot_general | solution.py:126
  481.5 6.6 fusion.9
  488.4 2.1 convolution_convert_fusion
  490.6 30.1 %reduce-scatter.9.cloned.1.call-done = bf16[32,3072]{1,0:T(8,128)(2,1)} async-done(((bf16[256,3072]{1,0:T(8,128)(2,1)}), bf16[32,3072]{1,0:T(8,128)(2,1)}) %reduce-scatter.9.cloned.1.call-update) | async-done | bytes 196624 | tf_op jit(solution)/shard_map/reduce_scatter | solution.py:43
  520.8 27.9 %all-gather.18.cloned.1.call-done = bf16[256,3072]{1,0:T(8,128)(2,1)} async-done(((bf16[32,3072]{1,0:T(8,128)(2,1)}), bf16[256,3072]{1,0:T(8,128)(2,1)}) %all-gather.18.cloned.1.call-update) | async-done | bytes 1572880 | tf_op jit(solution)/shard_map/all_gather | solution.py:44
  548.7 2.7 fusion.112
  551.5 1.7 copy-done.3
  553.6 13.7 %fusion.25 = bf16[256,3072]{1,0:T(8,128)(2,1)} fusion(bf16[3072,3072]{1,0:T(8,128)(2,1)} %all-gather.12.cloned.1.call-done, f32[256,3072]{1,0:T(8,128)} %copy-done.3, f32[256]{0:T(256)S(1)} %add_rsqrt_fusion.1, f32[256]{0:T(256)S(1)} %broadcast_multiply_fusion.1, f32[3072]{0:T(1024)S(1)} %copy-done.34), kind=kOutput, calls=%fused_computation.27 | convolution fusion | flops 4839309312 | bytes 23607296 | tf_op jit(solution)/shard_map/dot_general | solution.py:161
  567.4 30.2 %reduce-scatter.11.cloned.1.call-done = bf16[32,3072]{1,0:T(8,128)(2,1)} async-done(((bf16[256,3072]{1,0:T(8,128)(2,1)}), bf16[32,3072]{1,0:T(8,128)(2,1)}) %reduce-scatter.11.cloned.1.call-update) | async-done | bytes 196624 | tf_op jit(solution)/shard_map/reduce_scatter | solution.py:43
  597.6 28.0 %all-gather.20.cloned.1.call-done = bf16[256,3072]{1,0:T(8,128)(2,1)} async-done(((bf16[32,3072]{1,0:T(8,128)(2,1)}), bf16[256,3072]{1,0:T(8,128)(2,1)}) %all-gather.20.cloned.1.call-update) | async-done | bytes 1572880 | tf_op jit(solution)/shard_map/all_gather | solution.py:44
  625.5 2.9 fusion.77
  630.1 0.8 fusion.57
  630.9 3.2 collective-permute-start.1
  634.1 0.7 collective-permute-done.1
  634.9 1.8 collective-permute-start.2
  636.7 1.7 collective-permute-done.2
  638.4 3.1 collective-permute-start.3
  641.4 2.1 collective-permute-done.3
  643.5 2.9 collective-permute-start.4
  646.5 1.7 collective-permute-done.4
  648.1 3.2 collective-permute-start.5
  651.3 1.7 collective-permute-done.5
  653.0 0.7 convert_element_type.160
  (119 shorter events, 11.7 us)
Async XLA Ops:
  6.5 113.4 %copy-start = (bf16[384,3072]{1,0:T(8,128)(2,1)S(1)}, bf16[384,3072]{1,0:T(8,128)(2,1)}, u32[]{:S(2)}) copy-start(bf16[384,3072]{1,0:T(8,128)(2,1)} %param.21) | copy-start | bytes 7077892
  6.5 6.2 copy-start.20
  6.5 6.2 copy-start.17
  6.5 79.4 %all-gather.8.cloned.1.call-start = ((), (), s32[]{:S(2)}) async-start(), calls=%async_computation.4 | async-start | bytes 6684672 | tf_op jit(solution)/shard_map/all_gather | solution.py:29
  12.7 1.2 copy-start.9
  12.7 1.7 copy-start.11
  14.4 1.7 copy-start.5
  14.4 0.7 copy-start.25
  14.9 2.3 copy-start.30
  17.2 3.3 copy-start.18
  17.2 2.2 copy-start.32
  21.3 131.0 %reduce-scatter.5.cloned.1.call-start = ((), (), s32[]{:S(2)}) async-start(), calls=%async_computation.5 | async-start | bytes 1769472 | tf_op jit(solution)/shard_map/reduce_scatter | solution.py:43
  94.7 6.4 copy-start.29
  94.7 8.0 %copy-start.24 = (bf16[256,384]{1,0:T(8,128)(2,1)S(1)}, bf16[256,384]{1,0:T(8,128)(2,1)}, u32[]{:S(2)}) copy-start(bf16[256,384]{1,0:T(8,128)(2,1)} %get-tuple-element.47) | copy-start | bytes 589828 | tf_op jit(solution)/shard_map/cond
  102.9 9.7 %copy-start.15 = (bf16[4096,384]{0,1:T(8,128)(2,1)S(1)}, bf16[4096,384]{0,1:T(8,128)(2,1)}, u32[]{:S(2)}) copy-start(bf16[4096,384]{0,1:T(8,128)(2,1)} %get-tuple-element.59) | copy-start | bytes 9437188 | tf_op jit(solution)/shard_map/cond
  102.9 9.7 %copy-start.22 = (pred[256,4096]{1,0:T(8,128)(4,1)S(1)}, pred[256,4096]{1,0:T(8,128)(4,1)}, u32[]{:S(2)}) copy-start(pred[256,4096]{1,0:T(8,128)(4,1)} %broadcast_compare_fusion) | copy-start | bytes 3145732 | tf_op jit(solution)/shard_map/cond
  122.2 58.1 %all-gather.10.cloned.1.call-start = ((), (), s32[]{:S(2)}) async-start(), calls=%async_computation.6 | async-start | bytes 1769472 | tf_op jit(solution)/shard_map/all_gather | solution.py:44
  152.3 151.7 %all-gather.12.cloned.1.call-start = ((), (), s32[]{:S(2)}) async-start(), calls=%async_computation.7 | async-start | bytes 20054016 | tf_op jit(solution)/shard_map/all_gather | solution.py:18
  154.8 193.1 %reduce-scatter.7.cloned.1.call-start = ((), (), s32[]{:S(2)}) async-start(), calls=%async_computation.8 | async-start | bytes 1769472 | tf_op jit(solution)/shard_map/reduce_scatter | solution.py:43
  183.0 1.7 copy-start.1
  183.0 121.0 %copy-start.34 = (f32[3072]{0:T(1024)S(1)}, f32[3072]{0:T(1024)}, u32[]{:S(2)}) copy-start(f32[3072]{0:T(1024)} %param.26) | copy-start | bytes 36868
  317.8 57.9 %all-gather.14.cloned.1.call-start = ((), (), s32[]{:S(2)}) async-start(), calls=%async_computation.9 | async-start | bytes 1769472 | tf_op jit(solution)/shard_map/all_gather | solution.py:44
  347.9 107.5 %all-gather.16.cloned.1.call-start = ((), (), s32[]{:S(2)}) async-start(), calls=%async_computation.10 | async-start | bytes 6684672 | tf_op jit(solution)/shard_map/all_gather | solution.py:29
  375.7 3.3 copy-start.2
  375.7 3.8 copy-start.7
  378.6 1.6 copy-start.13
  378.6 1.6 copy-start.27
  380.3 4.8 copy-start.10
  380.3 4.8 copy-start.12
  380.3 4.8 copy-start.21
  381.1 4.0 collective-permute-start
  385.8 1.6 copy-start.6
  385.8 0.7 copy-start.26
  386.3 2.3 copy-start.31
  388.6 3.3 copy-start.19
  388.6 2.2 copy-start.33
  391.9 63.6 %copy-start.28 = (s32[256]{0:T(256)S(1)}, s32[256]{0:T(256)}, u32[]{:S(2)}) copy-start(s32[256]{0:T(256)} %iota_add_fusion) | copy-start | bytes 3076
  392.7 128.1 %reduce-scatter.9.cloned.1.call-start = ((), (), s32[]{:S(2)}) async-start(), calls=%async_computation.11 | async-start | bytes 1769472 | tf_op jit(solution)/shard_map/reduce_scatter | solution.py:43
  472.5 9.1 %copy-start.16 = (bf16[4096,384]{0,1:T(8,128)(2,1)S(1)}, bf16[4096,384]{0,1:T(8,128)(2,1)}, u32[]{:S(2)}) copy-start(bf16[4096,384]{0,1:T(8,128)(2,1)} %get-tuple-element.63) | copy-start | bytes 9437188 | tf_op jit(solution)/shard_map/cond
  472.5 9.1 %copy-start.23 = (pred[256,4096]{1,0:T(8,128)(4,1)S(1)}, pred[256,4096]{1,0:T(8,128)(4,1)}, u32[]{:S(2)}) copy-start(pred[256,4096]{1,0:T(8,128)(4,1)} %broadcast_compare_fusion.1) | copy-start | bytes 3145732 | tf_op jit(solution)/shard_map/cond
  490.6 58.1 %all-gather.18.cloned.1.call-start = ((), (), s32[]{:S(2)}) async-start(), calls=%async_computation.12 | async-start | bytes 1769472 | tf_op jit(solution)/shard_map/all_gather | solution.py:44
  520.8 76.8 %reduce-scatter.11.cloned.1.call-start = ((), (), s32[]{:S(2)}) async-start(), calls=%async_computation.13 | async-start | bytes 1769472 | tf_op jit(solution)/shard_map/reduce_scatter | solution.py:43
  551.5 1.7 copy-start.3
  567.4 58.2 %all-gather.20.cloned.1.call-start = ((), (), s32[]{:S(2)}) async-start(), calls=%async_computation.14 | async-start | bytes 1769472 | tf_op jit(solution)/shard_map/all_gather | solution.py:44
  625.5 3.3 copy-start.4
  625.5 3.8 copy-start.8
  628.4 1.6 copy-start.14
  630.9 3.9 collective-permute-start.1
  634.9 3.4 collective-permute-start.2
  638.4 5.2 collective-permute-start.3
  643.5 4.6 collective-permute-start.4
  648.1 4.8 collective-permute-start.5
Sparse Core Ops, SparseCore 0:
  21.4 64.4 all-gather.7
  122.3 29.9 reduce-scatter.4
  154.0 26.2 all-gather.9
  182.3 121.6 all-gather.11
  317.9 29.9 reduce-scatter.6
  349.4 26.2 all-gather.13
  392.8 62.6 all-gather.15
  490.7 29.9 reduce-scatter.8
  522.4 26.2 all-gather.17
  567.5 30.0 reduce-scatter.10
  599.3 26.2 all-gather.19
where the time goes:
time: 674 us; the launch traced here: 661 us
  waiting for transfers between devices  476 us (71%)
  matrix products  77.6 us (12%)
  local copies, waits for them, and re-layouts  42.8 us (6%)
  other arithmetic  31.1 us (5%)
  starting transfers between devices  18.1 us (3%)
  between operations  14.7 us (2%)
    reduce_scatter x4, waiting for transfers between devices, sum_by_parts(): own = lax.psum_scatter(padded, axis, scatter_dimension=0, tiled=True)  120 us
    all_gather x2, waiting for transfers between devices, in_one_piece(): whole = lax.all_gather(both, axis, axis=dim, tiled=True)  119 us
    all_gather x1, waiting for transfers between devices, rows_first(): whole, at, done = (lax.all_gather(both, axis, axis=0, tiled=True), 0, [])  119 us
    all_gather x4, waiting for transfers between devices, sum_by_parts(): whole = lax.all_gather(own, axis, axis=0, tiled=True)  109 us
    dot_general x2, matrix products, per_device(): jnp.dot(hidden, down_full, preferred_element_type=jnp.float32)  27.4 us
    dot_general x2, matrix products, update(): jnp.einsum('qhd,khd->hqk', queries, block_keys.reshape(attend_span_rows,...  18.8 us
    another operation x4, local copies, waits for them, and re-layouts  17.9 us
  transfers between devices with their start and end apart: 17, of which 17 were waited for; matrix products, arithmetic and copies ran while one was open for 2% of the time, Pallas kernels for 0%

commit v1 on v0

v1 whole, which is shorter than its diff:
```python
import functools

import jax
import jax.numpy as jnp
from jax import lax
from jax.experimental import pallas as pl
from jax.experimental.pallas import tpu as pltpu
from jax.sharding import PartitionSpec as P

D = 3072
HALF = D // 2
HEAD_DIM = 128
C = 128
ITERS = 2
EPSILON = 1e-05
KEY_BLOCK = 512
BF16 = jnp.bfloat16
F32 = jnp.float32


def split_two(value):
    high = lax.reduce_precision(value, 8, 7)
    return high.astype(BF16), (value - high).astype(BF16)


def dot(left, right):
    return jnp.dot(left, right, preferred_element_type=F32)


def dot_t(left, right):
    return lax.dot_general(left, right, (((1,), (1,)), ((), ())), preferred_element_type=F32)


def layer_norm(stream, gain):
    center = stream - jnp.mean(stream, axis=-1, keepdims=True)
    spread = jnp.mean(center * center, axis=-1, keepdims=True)
    return center * lax.rsqrt(spread + EPSILON) * gain


def frequencies():
    return jnp.exp(-jnp.log(10000.0) * 2.0 * jnp.arange(HALF).astype(F32) / D)


def embed_kernel(
    rows, turn_ref, base_ref, gain_ref, wq_ref, wk_ref, wv_ref, win_ref, gw_ref, ws_ref,
    ek_ref, ev_ref, h_ref, n_ref, eq_ref, scaled, high, low,
):
    block = pl.program_id(0)
    me = lax.axis_index("seq")
    total = jnp.zeros((rows, 1), F32)
    width = 512
    for at in range(0, HALF, width):
        cols = slice(at, at + width)
        sin_a, cos_a = turn_ref[0, 0:1, cols], turn_ref[0, 1:2, cols]
        sin_b, cos_b = base_ref[0, :, cols], base_ref[1, :, cols]
        for part, offset in (
            (sin_a * cos_b + cos_a * sin_b, 0),
            (cos_a * cos_b - sin_a * sin_b, HALF),
        ):
            into = slice(offset + at, offset + at + width)
            top = part.astype(BF16)
            high[:, into] = top
            low[:, into] = (part - top.astype(F32)).astype(BF16)
            scaled[:, into] = (part * gain_ref[:, into]).astype(BF16)
            total = total + jnp.sum(part, axis=1, keepdims=True)
    mean = total * (1.0 / D)
    ek_ref[...] = dot(scaled[...], wk_ref[...]) - mean * gw_ref[1:2, :]
    ev_ref[...] = dot(scaled[...], wv_ref[...]) - mean * gw_ref[2:3, :]
    h_ref[...] = dot_t(high[...], win_ref[...]) + dot_t(low[...], win_ref[...]) - mean * ws_ref[...]
    n_ref[...] = HALF - D * mean * mean

    @pl.when(block == me)
    def _():
        eq_ref[...] = dot(scaled[...], wq_ref[...]) - mean * gw_ref[0:1, :]


def embed_all(rows, blocks, gain, w_query, w_key, w_value, w_in, gw, w_sum):
    freq = frequencies()
    turn = (jnp.arange(blocks, dtype=F32) * rows)[:, None] * freq[None, :]
    turn = jnp.stack([jnp.sin(turn), jnp.cos(turn)], axis=1)
    base = jnp.arange(rows, dtype=F32)[:, None] * freq[None, :]
    base = jnp.stack([jnp.sin(base), jnp.cos(base)], axis=0)
    width = w_key.shape[1]
    whole = pl.BlockSpec(memory_space=pltpu.VMEM)
    length = rows * blocks
    return pl.pallas_call(
        functools.partial(embed_kernel, rows),
        grid=(blocks,),
        in_specs=[pl.BlockSpec((1, 2, HALF), lambda i: (i, 0, 0))] + [whole] * 8,
        out_specs=[
            pl.BlockSpec((rows, width), lambda i: (i, 0)),
            pl.BlockSpec((rows, width), lambda i: (i, 0)),
            pl.BlockSpec((rows, C), lambda i: (i, 0)),
            pl.BlockSpec((rows, 1), lambda i: (i, 0)),
            pl.BlockSpec((rows, width), lambda i: (0, 0)),
        ],
        out_shape=[
            jax.ShapeDtypeStruct((length, width), F32),
            jax.ShapeDtypeStruct((length, width), F32),
            jax.ShapeDtypeStruct((length, C), F32),
            jax.ShapeDtypeStruct((length, 1), F32),
            jax.ShapeDtypeStruct((rows, width), F32),
        ],
        scratch_shapes=[pltpu.VMEM((rows, D), BF16)] * 3,
        compiler_params=pltpu.CompilerParams(vmem_limit_bytes=48 << 20),
        cost_estimate=pl.CostEstimate(
            flops=2 * length * D * (2 * width + 2 * C),
            bytes_accessed=4 * length * 2 * width,
            transcendentals=0,
        ),
        name="embed_all",
    )(turn, base, gain, w_query, w_key, w_value, w_in, gw, w_sum)


def attend_kernel(
    rows, heads, x_ref, ek_ref, ev_ref, h_ref, n_ref, eq_ref, aq_ref, ak_ref, av_ref, g_ref,
    out_ref, queries, acc, sums,
):
    block = pl.program_id(0)
    me = lax.axis_index("seq")

    def scale_of(x, h, n):
        twice = jnp.concatenate([x, x], axis=1)
        quad = jnp.sum(x.astype(F32) * (dot(twice, g_ref[...]) + 2.0 * h), axis=1, keepdims=True)
        return twice, lax.rsqrt(jnp.maximum(quad + n, 0.0) * (1.0 / D) + EPSILON)

    @pl.when(block == 0)
    def _():
        own = pl.ds(pl.multiple_of(me * rows, rows), rows)
        twice, scale = scale_of(x_ref[own, :], h_ref[own, :], n_ref[own, :])
        value = (dot(twice, aq_ref[...]) + eq_ref[...]) * (scale * HEAD_DIM**-0.5)
        queries[...] = value.astype(BF16)
        acc[...] = jnp.zeros_like(acc)
        sums[...] = jnp.zeros_like(sums)

    def step(masked):
        here = pl.ds(pl.multiple_of(block * KEY_BLOCK, KEY_BLOCK), KEY_BLOCK)
        twice, scale = scale_of(x_ref[here, :], h_ref[here, :], n_ref[here, :])
        keys = ((dot(twice, ak_ref[...]) + ek_ref[...]) * scale).astype(BF16)
        values = ((dot(twice, av_ref[...]) + ev_ref[...]) * scale).astype(BF16)
        if masked:
            shape = (rows, KEY_BLOCK)
            row = me * rows + lax.broadcasted_iota(jnp.int32, shape, 0)
            col = block * KEY_BLOCK + lax.broadcasted_iota(jnp.int32, shape, 1)
            seen = col <= row
        for head in range(heads):
            cols = slice(head * HEAD_DIM, (head + 1) * HEAD_DIM)
            scores = dot_t(queries[:, cols], keys[:, cols])
            if masked:
                weights = jnp.where(seen, jnp.exp(jnp.where(seen, scores, 0.0)), 0.0)
            else:
                weights = jnp.exp(scores)
            part = weights[:, :HEAD_DIM]
            for at in range(HEAD_DIM, KEY_BLOCK, HEAD_DIM):
                part = part + weights[:, at : at + HEAD_DIM]
            sums[:, cols] += part
            acc[:, cols] += dot(weights.astype(BF16), values[:, cols])

    last = (me * rows + rows - 1) // KEY_BLOCK

    @pl.when(block < last)
    def _():
        step(False)

    @pl.when(block == last)
    def _():
        step(True)

    @pl.when(block == pl.num_programs(0) - 1)
    def _():
        for head in range(heads):
            cols = slice(head * HEAD_DIM, (head + 1) * HEAD_DIM)
            total = jnp.sum(sums[:, cols], axis=1, keepdims=True)
            out_ref[:, cols] = (acc[:, cols] / total).astype(BF16)


def attend(rows, x, ek, ev, h, n, eq, aq, ak, av, gram):
    length, width = ek.shape
    heads = width // HEAD_DIM
    whole = pl.BlockSpec(memory_space=pltpu.VMEM)
    tile = pl.BlockSpec((KEY_BLOCK, width), lambda i: (i, 0))
    return pl.pallas_call(
        functools.partial(attend_kernel, rows, heads),
        grid=(length // KEY_BLOCK,),
        in_specs=[whole, tile, tile] + [whole] * 7,
        out_specs=whole,
        out_shape=jax.ShapeDtypeStruct((rows, width), BF16),
        scratch_shapes=[
            pltpu.VMEM((rows, width), BF16),
            pltpu.VMEM((rows, width), F32),
            pltpu.VMEM((rows, width), F32),
        ],
        compiler_params=pltpu.CompilerParams(vmem_limit_bytes=40 << 20),
        cost_estimate=pl.CostEstimate(
            flops=4 * length * rows * width * 2, bytes_accessed=8 * length * width, transcendentals=0
        ),
        name="attend",
    )(x, ek, ev, h, n, eq, aq, ak, av, gram)


def per_device(
    latent, w_in, w_query, w_key, w_value, w_attn_out, w_up, w_down, w_final,
    gain_attn, gain_mlp, gain_final,
):
    seq_count, head_count = lax.axis_size("seq"), lax.axis_size("head")
    me, mine = lax.axis_index("seq"), lax.axis_index("head")
    rows = latent.shape[0]
    share = rows // head_count
    length = rows * seq_count
    first = me * rows + mine * share

    latents = lax.all_gather(latent, "seq", axis=0, tiled=True)
    up_full = lax.all_gather(w_up, "seq", axis=0, tiled=True)
    down_full = lax.all_gather(w_down.T, "seq", axis=0, tiled=True)

    w_wide = w_in.astype(F32)
    center = w_wide - jnp.mean(w_wide, axis=1, keepdims=True)
    gram = lax.dot_general(
        center, center, (((1,), (1,)), ((), ())), precision=lax.Precision.HIGHEST
    )
    gram = jnp.concatenate(split_two(gram), axis=0)
    scaled = jnp.concatenate(split_two(center * gain_attn), axis=0)
    stacks, sums = [], []
    gain_parts = jnp.concatenate(split_two(gain_attn[None, :]), axis=0)
    for weight in (w_query, w_key, w_value):
        both = dot(scaled, weight)
        stacks.append(jnp.concatenate(split_two(both[:C] + both[C:]), axis=0))
        sums.append(jnp.sum(dot(gain_parts, weight), axis=0))
    gw = jnp.stack(sums)
    w_sum = jnp.sum(w_wide, axis=1)[None, :]
    ek, ev, h, n, eq = embed_all(
        rows, seq_count, gain_attn[None, :], w_query, w_key, w_value, w_in, gw, w_sum
    )

    angles = (first + jnp.arange(share)).astype(F32)[:, None] * frequencies()[None, :]
    embedding = jnp.concatenate([jnp.sin(angles), jnp.cos(angles)], axis=1)
    ahead = lax.dynamic_slice_in_dim(
        jnp.concatenate([latents[1:], latents[:1]], axis=0), first, share, 0
    )
    x = latents.astype(BF16)
    for step_index in range(ITERS):
        own = lax.dynamic_slice_in_dim(x, first, share, 0)
        stream_in = dot(own, w_in) + embedding
        attended = attend(rows, x, ek, ev, h, n, eq, *stacks, gram)
        term = dot(attended, w_attn_out).astype(BF16)
        stream_attn = stream_in + lax.psum_scatter(
            term, "head", scatter_dimension=0, tiled=True
        ).astype(F32)
        normed = layer_norm(stream_attn, gain_mlp).astype(BF16)
        normed = lax.all_gather(normed, "head", axis=0, tiled=True)
        hidden = jax.nn.gelu(dot(normed, up_full), approximate=True).astype(BF16)
        term = dot_t(hidden, down_full).astype(BF16)
        stream_mlp = stream_attn + lax.psum_scatter(
            term, "head", scatter_dimension=0, tiled=True
        ).astype(F32)
        params = dot(layer_norm(stream_mlp, gain_final).astype(BF16), w_final)
        following = ahead * jnp.exp(jnp.tanh(params[:, C:])) + params[:, :C]
        following = lax.all_gather(following.astype(BF16), ("seq", "head"), axis=0, tiled=True)
        x = jnp.concatenate([latents[:1].astype(BF16), following[:-1]], axis=0)
    mirrored = lax.dynamic_slice_in_dim(x, (seq_count - 1 - me) * rows, rows, 0)
    return mirrored[::-1].astype(F32)


def solution(mesh):
    in_specs = (
        P("seq", None),
        P(),
        P(None, "head"),
        P(None, "head"),
        P(None, "head"),
        P("head", None),
        P("seq", "head"),
        P("head", "seq"),
        P(),
        P(),
        P(),
        P(),
    )
    return jax.shard_map(
        per_device, mesh=mesh, in_specs=in_specs, out_specs=P("seq", None), check_vma=False
    )
```

time: 674 us -> 648 us (0.961); the launches traced: 661 us -> 642 us
  Pallas kernels: 0 us -> 63.8 us
  matrix products: 77.6 us -> 43.4 us
  local copies, waits for them, and re-layouts: 42.8 us -> 22.5 us
  starting transfers between devices: 18.1 us -> 0.41 us
  waiting for transfers between devices: 476 us -> 467 us
    pallas_call x0 -> x3, Pallas kernels: none -> 63.8 us  [the longest x1 49.7 us: embed_all(): pl.pallas_call(functools.partial(embed_kernel, rows), grid=(blocks,), in_...]
    dot_general x16 -> x15, matrix products: 64.4 us -> 43.4 us  [the longest x2 26.3 us: dot_t(): lax.dot_general(left, right, (((1,), (1,)), ((), ())), preferred_element_...]
    another operation x4 -> x3, local copies, waits for them, and re-layouts: 17.9 us -> 0.01 us  [per_device(): gw = jnp.stack(sums)]
    ppermute x6 -> x0, starting transfers between devices: 17.5 us -> none  [the longest x4 11 us: swapped(): return lax.ppermute(block, axis, route)]
    cond x2 -> x0, matrix products: 13.1 us -> none  [per_device(): lax.cond(jnp.min(attend_key_positions) <= query_last, update, lambda stat...]
    split x2 -> x0, local copies, waits for them, and re-layouts: 12.7 us -> none  [in_one_piece(): jnp.split(whole, [sum(widths[:k]) for k in range(1, len(widths))], axis=a...]
    all_gather x7, waiting for transfers between devices: 347 us -> 337 us  [the longest x2 131 us: per_device(): lax.all_gather(following.astype(BF16), ('seq', 'head'), axis=0, tiled=True)]
    reduce_sum x4 -> x2, other arithmetic: 11.3 us -> 2.41 us  [layer_norm(): center = stream - jnp.mean(stream, axis=-1, keepdims=True)]
  transfers between devices with their start and end apart: 17 -> 11, of which waited for: 17 -> 10; matrix products, arithmetic and copies ran while one was open for 2% -> 4% of each run, Pallas kernels for 0% -> 8%
where the time goes in v1:
time: 648 us; the launch traced here: 642 us
  waiting for transfers between devices  467 us (72%)
  Pallas kernels  63.8 us (10%)
  matrix products  43.4 us (7%)
  other arithmetic  30.7 us (5%)
  local copies, waits for them, and re-layouts  22.5 us (3%)
  between operations  14.1 us (2%)
    all_gather x2, waiting for transfers between devices, per_device(): lax.all_gather(following.astype(BF16), ('seq', 'head'), axis=0, tiled=True)  131 us
    reduce_scatter x4, waiting for transfers between devices, per_device(): lax.psum_scatter(term, 'head', scatter_dimension=0, tiled=True).astype(F32)  128 us
    all_gather x1, waiting for transfers between devices, per_device(): up_full = lax.all_gather(w_up, 'seq', axis=0, tiled=True)  77.4 us
    all_gather x1, waiting for transfers between devices, per_device(): down_full = lax.all_gather(w_down.T, 'seq', axis=0, tiled=True)  77.3 us
    all_gather x2, waiting for transfers between devices, per_device(): normed = lax.all_gather(normed, 'head', axis=0, tiled=True)  51.5 us
    pallas_call x1, Pallas kernels, embed_all(): pl.pallas_call(functools.partial(embed_kernel, rows), grid=(blocks,), in_...  49.7 us
    dot_general x2, matrix products, dot_t(): lax.dot_general(left, right, (((1,), (1,)), ((), ())), preferred_element_...  26.3 us
    unnamed x64, local copies, waits for them, and re-layouts  18.7 us
  transfers between devices with their start and end apart: 11, of which 10 were waited for; matrix products, arithmetic and copies ran while one was open for 4% of the time, Pallas kernels for 8%

profile of v1, /device:TPU:1, one launch (start us, length us, event | category | flops | bytes accessed | tf_op | source)
XLA Modules:
  0.0 641.6 jit_solution(10344467585086872915)
XLA Ops:
  6.5 0.7 all-gather.8.cloned.1.call-update
  7.3 1.5 convert_reduce_fusion
  8.8 0.7 reduce-precision_convert_fusion.5
  9.5 1.5 reduce-precision_convert_fusion
  11.1 1.0 fusion.35
  12.1 0.6 copy-done.23
  12.7 1.0 fusion.36
  14.7 1.2 copy-done.25
  16.3 1.0 fusion.34
  17.5 1.7 reduce-precision_convert_fusion.4
  19.3 0.6 pad_maximum_fusion.11.g_ref
  20.0 0.7 pad_maximum_fusion.8
  20.7 3.2 multiply_sine_fusion.1
  24.1 5.5 fusion.22
  29.6 1.8 pad_maximum_fusion.base_ref
  31.5 49.7 %embed_all.1 = (f32[4096,384]{1,0:T(8,128)}, f32[4096,384]{1,0:T(8,128)}, f32[4096,128]{1,0:T(8,128)S(1)}, f32[4096,1]{1,0:T(8,128)S(1)}, f32[256,384]{1,0:T(8,128)S(1)}) custom-call(f32[16,2,1536]{2,1,0:T(2,128)S(1)} %pad_maximum_fusion.7.turn_ref, f32[2,256,1536]{2,1,0:T(8,128)} %pad_maximum_fusion.base_ref, f32[1,3072]{1,0:T(1,128)S(1)} %bitcast.25, ...), custom_call_target="tpu_custom_call" | custom-call | flops 25769803776 | bytes 12582912 | tf_op jit(solution)/shard_map/embed_all/pallas_call | solution.py:86
  81.2 1.3 copy-done.4
  82.5 1.3 copy-done.7
  83.8 0.8 copy-done.13
  84.6 1.8 convert_element_type.127.x_ref
  86.9 2.8 copy-done.1
  89.7 1.6 copy-done.8
  91.3 7.0 %attend.2 = bf16[256,384]{1,0:T(8,128)(2,1)S(1)} custom-call(bf16[4096,128]{1,0:T(8,128)(2,1)S(1)} %convert_element_type.127.x_ref, f32[4096,384]{1,0:T(8,128)S(1)} %copy-done.1, f32[4096,384]{1,0:T(8,128)} %get-tuple-element.11.ev_ref, f32[4096,128]{1,0:T(8,128)S(1)} %copy-done.5, f32[4096,1]{1,0:T(8,128)S(1)} %copy-done.8, f32[256,384]{1,0:T(8,128)S(1)} %copy-done.14, ...), custom_call_target="tpu_custom_call" | custom-call | flops 3221225472 | bytes 12582912 | tf_op jit(solution)/shard_map/attend/pallas_call | solution.py:182
  98.3 2.2 convolution_convert_fusion.3
  100.6 1.5 multiply_sine_fusion
  102.1 37.6 %reduce-scatter.5.cloned.1.call-done = bf16[32,3072]{1,0:T(8,128)(2,1)} async-done(((bf16[256,3072]{1,0:T(8,128)(2,1)}), bf16[32,3072]{1,0:T(8,128)(2,1)}) %reduce-scatter.5.cloned.1.call-update) | async-done | bytes 196624 | tf_op jit(solution)/shard_map/reduce_scatter | solution.py:246
  139.7 1.5 fusion.78
  141.5 0.5 copy-done.19
  142.0 0.8 multiply_convert_fusion.3
  142.9 0.5 all-gather.12.cloned.1.call-update
  143.4 0.5 all-gather.14.cloned.1.call-update
  144.0 25.2 %all-gather.10.cloned.1.call-done = bf16[256,3072]{1,0:T(8,128)(2,1)} async-done(((bf16[32,3072]{1,0:T(8,128)(2,1)}), bf16[256,3072]{1,0:T(8,128)(2,1)}) %all-gather.10.cloned.1.call-update) | async-done | bytes 1572880 | tf_op jit(solution)/shard_map/all_gather | solution.py:250
  169.2 77.4 %all-gather.12.cloned.1.call-done = bf16[3072,1536]{1,0:T(8,128)(2,1)} async-done(((bf16[192,1536]{1,0:T(8,128)(2,1)}), bf16[3072,1536]{1,0:T(8,128)(2,1)}) %all-gather.12.cloned.1.call-update) | async-done | bytes 9437200 | tf_op jit(solution)/shard_map/all_gather | solution.py:213
  246.6 77.3 %all-gather.14.cloned.1.call-done = bf16[3072,1536]{1,0:T(8,128)(2,1)} async-done(((bf16[192,1536]{1,0:T(8,128)(2,1)}), bf16[3072,1536]{1,0:T(8,128)(2,1)}) %all-gather.14.cloned.1.call-update) | async-done | bytes 9437200 | tf_op jit(solution)/shard_map/all_gather | solution.py:214
  324.0 13.1 %convolution_convert_fusion.2 = bf16[256,3072]{1,0:T(8,128)(2,1)} fusion(bf16[3072,1536]{1,0:T(8,128)(2,1)} %all-gather.14.cloned.1.call-done, bf16[256,3072]{1,0:T(8,128)(2,1)} %all-gather.10.cloned.1.call-done, bf16[3072,1536]{1,0:T(8,128)(2,1)} %all-gather.12.cloned.1.call-done), kind=kOutput, calls=%fused_computation.2 | convolution fusion | flops 4836163584 | bytes 22020096 | tf_op jit(solution)/shard_map/dot_general | solution.py:31
  337.2 3.0 slice.59
  340.2 27.1 %reduce-scatter.7.cloned.1.call-done = bf16[32,3072]{1,0:T(8,128)(2,1)} async-done(((bf16[256,3072]{1,0:T(8,128)(2,1)}), bf16[32,3072]{1,0:T(8,128)(2,1)}) %reduce-scatter.7.cloned.1.call-update) | async-done | bytes 196624 | tf_op jit(solution)/shard_map/reduce_scatter | solution.py:253
  367.3 1.3 fusion.48
  368.7 1.3 multiply_reduce_fusion.2
  369.9 2.1 fusion.40
  372.0 0.6 fusion.56
  372.7 0.7 slice.123
  373.4 64.9 %all-gather.16.cloned.1.call-done = bf16[4096,128]{1,0:T(8,128)(2,1)} async-done(((bf16[32,128]{1,0:T(8,128)(2,1)}), bf16[4096,128]{1,0:T(8,128)(2,1)}) %all-gather.16.cloned.1.call-update) | async-done | bytes 1048592 | tf_op jit(solution)/shard_map/all_gather | solution.py:258
  438.4 1.6 pad_maximum_fusion.1.x_ref
  440.3 2.8 copy-done.2
  443.0 1.6 copy-done.9
  444.6 0.9 copy-done.12
  445.6 1.0 copy-done.15
  446.6 0.8 copy-done.17
  447.4 7.1 %attend.3 = bf16[256,384]{1,0:T(8,128)(2,1)S(1)} custom-call(bf16[4096,128]{1,0:T(8,128)(2,1)S(1)} %pad_maximum_fusion.1.x_ref, f32[4096,384]{1,0:T(8,128)S(1)} %copy-done.2, f32[4096,384]{1,0:T(8,128)} %get-tuple-element.11.ev_ref, f32[4096,128]{1,0:T(8,128)S(1)} %copy-done.6, f32[4096,1]{1,0:T(8,128)S(1)} %copy-done.9, f32[256,384]{1,0:T(8,128)S(1)} %copy-done.15, ...), custom_call_target="tpu_custom_call" | custom-call | flops 3221225472 | bytes 12582912 | tf_op jit(solution)/shard_map/attend/pallas_call | solution.py:182
  454.5 2.1 convolution_convert_fusion.1
  456.7 33.0 %reduce-scatter.9.cloned.1.call-done = bf16[32,3072]{1,0:T(8,128)(2,1)} async-done(((bf16[256,3072]{1,0:T(8,128)(2,1)}), bf16[32,3072]{1,0:T(8,128)(2,1)}) %reduce-scatter.9.cloned.1.call-update) | async-done | bytes 196624 | tf_op jit(solution)/shard_map/reduce_scatter | solution.py:246
  489.7 1.3 fusion.79
  491.8 0.8 multiply_convert_fusion.1
  492.6 26.3 %all-gather.18.cloned.1.call-done = bf16[256,3072]{1,0:T(8,128)(2,1)} async-done(((bf16[32,3072]{1,0:T(8,128)(2,1)}), bf16[256,3072]{1,0:T(8,128)(2,1)}) %all-gather.18.cloned.1.call-update) | async-done | bytes 1572880 | tf_op jit(solution)/shard_map/all_gather | solution.py:250
  518.9 13.2 %convolution_convert_fusion = bf16[256,3072]{1,0:T(8,128)(2,1)} fusion(bf16[3072,1536]{1,0:T(8,128)(2,1)} %all-gather.14.cloned.1.call-done, bf16[256,3072]{1,0:T(8,128)(2,1)} %all-gather.18.cloned.1.call-done, bf16[3072,1536]{1,0:T(8,128)(2,1)} %all-gather.12.cloned.1.call-done), kind=kOutput, calls=%fused_computation | convolution fusion | flops 4836163584 | bytes 22020096 | tf_op jit(solution)/shard_map/dot_general | solution.py:31
  532.2 30.2 %reduce-scatter.11.cloned.1.call-done = bf16[32,3072]{1,0:T(8,128)(2,1)} async-done(((bf16[256,3072]{1,0:T(8,128)(2,1)}), bf16[32,3072]{1,0:T(8,128)(2,1)}) %reduce-scatter.11.cloned.1.call-update) | async-done | bytes 196624 | tf_op jit(solution)/shard_map/reduce_scatter | solution.py:253
  562.4 1.1 fusion.49
  563.5 1.1 multiply_reduce_fusion
  564.7 1.9 fusion.41
  566.6 0.6 fusion.53
  567.3 65.6 %all-gather.20.cloned.1.call-done = bf16[4096,128]{1,0:T(8,128)(2,1)} async-done(((bf16[32,128]{1,0:T(8,128)(2,1)}), bf16[4096,128]{1,0:T(8,128)(2,1)}) %all-gather.20.cloned.1.call-update) | async-done | bytes 1048592 | tf_op jit(solution)/shard_map/all_gather | solution.py:258
  632.9 0.9 fusion.50
  633.9 0.7 convert_element_type.161
  (102 shorter events, 4.2 us)
Async XLA Ops:
  6.5 91.8 %copy-start = (bf16[384,3072]{1,0:T(8,128)(2,1)S(1)}, bf16[384,3072]{1,0:T(8,128)(2,1)}, u32[]{:S(2)}) copy-start(bf16[384,3072]{1,0:T(8,128)(2,1)} %param.17) | copy-start | bytes 7077892
  6.5 78.1 %all-gather.8.cloned.1.call-start = ((), (), s32[]{:S(2)}) async-start(), calls=%async_computation.4 | async-start | bytes 2228224 | tf_op jit(solution)/shard_map/all_gather | solution.py:212
  7.3 132.5 %reduce-scatter.5.cloned.1.call-start = ((), (), s32[]{:S(2)}) async-start(), calls=%async_computation.5 | async-start | bytes 1769472 | tf_op jit(solution)/shard_map/reduce_scatter | solution.py:246
  7.3 3.8 copy-start.24
  11.1 1.7 copy-start.23
  14.2 1.7 copy-start.25
  16.3 1.1 copy-start.3
  29.6 1.8 copy-start.18
  81.2 1.3 copy-start.4
  82.5 1.3 copy-start.7
  83.8 0.8 copy-start.13
  84.6 2.2 copy-start.5
  84.6 2.2 copy-start.11
  84.6 2.3 copy-start.14
  84.6 2.3 copy-start.16
  86.5 11.9 %copy-start.10 = (bf16[4096,128]{1,0:T(8,128)(2,1)}, bf16[4096,128]{1,0:T(8,128)(2,1)S(1)}, u32[]{:S(2)}) copy-start(bf16[4096,128]{1,0:T(8,128)(2,1)S(1)} %convert_element_type.127.x_ref) | copy-start | bytes 3145732
  86.9 2.8 copy-start.1
  89.7 1.6 copy-start.8
  100.5 68.7 %all-gather.10.cloned.1.call-start = ((), (), s32[]{:S(2)}) async-start(), calls=%async_computation.6 | async-start | bytes 1769472 | tf_op jit(solution)/shard_map/all_gather | solution.py:250
  102.1 39.9 %copy-start.30 = (f32[3072]{0:T(1024)S(1)}, f32[3072]{0:T(1024)}, u32[]{:S(2)}) copy-start(f32[3072]{0:T(1024)} %param.22) | copy-start | bytes 36868
  141.2 0.8 copy-start.19
  142.8 103.8 %all-gather.12.cloned.1.call-start = ((), (), s32[]{:S(2)}) async-start(), calls=%async_computation.7 | async-start | bytes 10027008 | tf_op jit(solution)/shard_map/all_gather | solution.py:213
  143.4 180.6 %all-gather.14.cloned.1.call-start = ((), (), s32[]{:S(2)}) async-start(), calls=%async_computation.8 | async-start | bytes 10027008 | tf_op jit(solution)/shard_map/all_gather | solution.py:214
  144.0 223.3 %reduce-scatter.7.cloned.1.call-start = ((), (), s32[]{:S(2)}) async-start(), calls=%async_computation.9 | async-start | bytes 1769472 | tf_op jit(solution)/shard_map/reduce_scatter | solution.py:253
  337.1 32.8 %copy-start.29 = (f32[3072]{0:T(1024)S(1)}, f32[3072]{0:T(1024)}, u32[]{:S(2)}) copy-start(f32[3072]{0:T(1024)} %param.23) | copy-start | bytes 36868
  337.1 101.2 %all-gather.16.cloned.1.call-start = ((), (), s32[]{:S(2)}) async-start(), calls=%async_computation.10 | async-start | bytes 1056768 | tf_op jit(solution)/shard_map/all_gather | solution.py:258
  340.2 31.8 %slice-start = ((f32[4096,128]{1,0:T(8,128)}), f32[1,128]{1,0:T(1,128)S(1)}, s32[]{:S(2)}) async-start(f32[4096,128]{1,0:T(8,128)} %all-gather.8.cloned.1.call-done), calls=%async_computation.15 | async-start | bytes 1024 | tf_op jit(solution)/shard_map/slice | solution.py:259
  367.3 4.7 copy-start.22
  372.7 117.0 %reduce-scatter.9.cloned.1.call-start = ((), (), s32[]{:S(2)}) async-start(), calls=%async_computation.11 | async-start | bytes 1769472 | tf_op jit(solution)/shard_map/reduce_scatter | solution.py:246
  438.4 1.9 copy-start.6
  440.3 2.8 copy-start.2
  443.0 1.6 copy-start.9
  444.6 0.9 copy-start.12
  445.6 1.0 copy-start.15
  446.6 0.8 copy-start.17
  456.6 33.1 %copy-start.26 = (f32[32,1536]{1,0:T(8,128)S(1)}, f32[32,1536]{1,0:T(8,128)}, u32[]{:S(2)}) copy-start(f32[32,1536]{1,0:T(8,128)} %get-tuple-element.29) | copy-start | bytes 589828
  456.6 33.1 %copy-start.27 = (f32[32,1536]{1,0:T(8,128)S(1)}, f32[32,1536]{1,0:T(8,128)}, u32[]{:S(2)}) copy-start(f32[32,1536]{1,0:T(8,128)} %get-tuple-element.30) | copy-start | bytes 589828
  456.6 62.3 %all-gather.18.cloned.1.call-start = ((), (), s32[]{:S(2)}) async-start(), calls=%async_computation.12 | async-start | bytes 1769472 | tf_op jit(solution)/shard_map/all_gather | solution.py:250
  489.7 2.1 copy-start.31
  491.0 0.8 copy-start.20
  492.6 69.9 %reduce-scatter.11.cloned.1.call-start = ((), (), s32[]{:S(2)}) async-start(), calls=%async_computation.13 | async-start | bytes 1769472 | tf_op jit(solution)/shard_map/reduce_scatter | solution.py:253
  532.1 30.3 %copy-start.21 = (f32[32,3072]{1,0:T(8,128)S(1)}, f32[32,3072]{1,0:T(8,128)}, u32[]{:S(2)}) copy-start(f32[32,3072]{1,0:T(8,128)} %copy-done.20) | copy-start | bytes 1179652
  532.2 34.5 %copy-start.28 = (f32[32,128]{1,0:T(8,128)S(1)}, f32[32,128]{1,0:T(8,128)}, u32[]{:S(2)}) copy-start(f32[32,128]{1,0:T(8,128)} %get-tuple-element.16) | copy-start | bytes 49156
  532.2 100.7 %all-gather.20.cloned.1.call-start = ((), (), s32[]{:S(2)}) async-start(), calls=%async_computation.14 | async-start | bytes 1056768 | tf_op jit(solution)/shard_map/all_gather | solution.py:258
Sparse Core Ops, SparseCore 0:
  9.5 46.6 all-gather.7
  100.7 39.0 reduce-scatter.4
  142.9 26.2 all-gather.9
  171.3 75.3 all-gather.11
  248.7 75.2 all-gather.13
  337.2 30.0 reduce-scatter.6
  372.8 65.5 all-gather.15
  456.7 32.8 reduce-scatter.8
  492.7 26.2 all-gather.17
  532.3 30.1 reduce-scatter.10
  567.4 65.4 all-gather.19
